TPU v7x, 16 devices: a whole 2x2x2 slice. The times are simulated.
16 devices in a mesh: ep: 16 (over z, y, x, core).
Axes of the slice: x: 2, y: 2, z: 2, core: 2. Of those that a mesh axis runs over, the one named last changes fastest.
Arguments:
- hidden: bfloat16 [32768, 1536], P('ep')
- grad_out: bfloat16 [32768, 1536], P('ep')
- routes: int32 [32768, 6], P('ep')
- w_router: bfloat16 [1536, 64], replicated
- w_one: bfloat16 [64, 1536, 512], P('ep')
- w_three: bfloat16 [64, 1536, 512], P('ep')
- w_two: bfloat16 [64, 512, 1536], P('ep')
- shared_one: bfloat16 [1536, 1024], replicated
- shared_three: bfloat16 [1536, 1024], replicated
- shared_two: bfloat16 [1024, 1536], replicated
Outputs:
- output 1: bfloat16 [32768, 1536], P('ep')
- output 2: bfloat16 [32768, 1536], P('ep')
- output 3: float32 [1536, 64], replicated
- output 4: bfloat16 [64, 1536, 512], P('ep')
- output 5: bfloat16 [64, 1536, 512], P('ep')
- output 6: bfloat16 [64, 512, 1536], P('ep')
- output 7: float32 [1536, 1024], replicated
- output 8: float32 [1536, 1024], replicated
- output 9: float32 [1024, 1536], replicated
All inputs are finite; a program needn't handle non-finite values.
Results may differ from a plain program's by a relative error of at most 0.00179.
Values are sent between devices in bfloat16 or wider.
A program may use at most 1 GiB of HBM per device.

v0:
```python
import jax
import jax.numpy as jnp
from jax import lax
from jax.sharding import PartitionSpec as P

ROUTE_SCALE = 2.5


def silu_parts(pre_act):
    sig_val = jax.nn.sigmoid(pre_act)
    return pre_act * sig_val, sig_val * (1.0 + pre_act * (1.0 - sig_val))


def router_weights(hidden, routes, w_router):
    logits = jnp.dot(hidden, w_router, preferred_element_type=jnp.float32)
    picked = jnp.take_along_axis(jax.nn.sigmoid(logits), routes, axis=1)
    pick_sum = jnp.sum(picked, axis=1, keepdims=True)
    return picked, pick_sum, ROUTE_SCALE * picked / pick_sum


def slot_tables(routes, weights, num_experts, capacity):
    tok_count = routes.shape[0]
    expert_ids = jnp.arange(num_experts, dtype=jnp.int32)
    hit_count = jnp.sum((routes[:, :, None] == expert_ids).astype(jnp.int32), axis=1)
    before = jnp.cumsum(hit_count, axis=0) - hit_count
    position = jnp.take_along_axis(before, routes, axis=1)
    slot_ids = jnp.where(position < capacity, routes * capacity + position, num_experts * capacity)
    token_ids = jnp.broadcast_to(jnp.arange(tok_count, dtype=jnp.int32)[:, None], routes.shape)
    flat_slots = slot_ids.reshape(-1)
    slot_token = jnp.full((num_experts * capacity,), tok_count, jnp.int32).at[flat_slots].set(token_ids.reshape(-1), mode='drop')
    slot_weight = jnp.zeros((num_experts * capacity,), jnp.float32).at[flat_slots].set(weights.reshape(-1), mode='drop')
    return slot_ids, slot_token, slot_weight


def router_grad_logits(route_dot, picked, pick_sum, weights, routes, num_experts):
    mean_term = jnp.sum(route_dot * weights, axis=1, keepdims=True) / ROUTE_SCALE
    grad_pick = ROUTE_SCALE / pick_sum * (route_dot - mean_term) * picked * (1.0 - picked)
    is_choice = routes[:, :, None] == jnp.arange(num_experts, dtype=jnp.int32)
    return jnp.sum(jnp.where(is_choice, grad_pick[:, :, None], 0.0), axis=1).astype(jnp.bfloat16)


def shared_forward(hidden, shared_one, shared_three, shared_two):
    pre_one = jnp.dot(hidden, shared_one, preferred_element_type=jnp.float32)
    pre_three = jnp.dot(hidden, shared_three, preferred_element_type=jnp.float32)
    act_one, dact_one = silu_parts(pre_one)
    mid_act = (act_one * pre_three).astype(jnp.bfloat16)
    return jnp.dot(mid_act, shared_two, preferred_element_type=jnp.float32), (pre_three, act_one, dact_one, mid_act)


def shared_backward(hidden, grad_out, saved_acts, shared_one, shared_three, shared_two):
    pre_three, act_one, dact_one, mid_act = saved_acts
    grad_mid = jnp.einsum('td,fd->tf', grad_out, shared_two, preferred_element_type=jnp.float32)
    grad_one = (grad_mid * pre_three * dact_one).astype(jnp.bfloat16)
    grad_three = (grad_mid * act_one).astype(jnp.bfloat16)
    wgrad_one = jnp.einsum('td,tf->df', hidden, grad_one, preferred_element_type=jnp.float32)
    wgrad_three = jnp.einsum('td,tf->df', hidden, grad_three, preferred_element_type=jnp.float32)
    wgrad_two = jnp.einsum('tf,td->fd', mid_act, grad_out, preferred_element_type=jnp.float32)
    dx_part = jnp.einsum('tf,df->td', grad_one, shared_one, preferred_element_type=jnp.float32) + jnp.einsum('tf,df->td', grad_three, shared_three, preferred_element_type=jnp.float32)
    return dx_part, wgrad_one, wgrad_three, wgrad_two


def expert_forward(in_rows, w_one, w_three, w_two):
    pre_one = jnp.einsum('secd,edf->secf', in_rows, w_one, preferred_element_type=jnp.float32)
    pre_three = jnp.einsum('secd,edf->secf', in_rows, w_three, preferred_element_type=jnp.float32)
    act_one, dact_one = silu_parts(pre_one)
    mid_act = (act_one * pre_three).astype(jnp.bfloat16)
    expert_out = jnp.einsum('secf,efd->secd', mid_act, w_two, preferred_element_type=jnp.float32).astype(jnp.bfloat16)
    return expert_out, (pre_three, act_one, dact_one, mid_act)


def expert_backward(in_rows, grad_rows, saved_acts, w_one, w_three, w_two):
    pre_three, act_one, dact_one, mid_act = saved_acts
    grad_mid = jnp.einsum('secd,efd->secf', grad_rows, w_two, preferred_element_type=jnp.float32)
    grad_one = (grad_mid * pre_three * dact_one).astype(jnp.bfloat16)
    grad_three = (grad_mid * act_one).astype(jnp.bfloat16)
    wgrad_two = jnp.einsum('secf,secd->efd', mid_act, grad_rows, preferred_element_type=jnp.float32)
    wgrad_one = jnp.einsum('secd,secf->edf', in_rows, grad_one, preferred_element_type=jnp.float32)
    wgrad_three = jnp.einsum('secd,secf->edf', in_rows, grad_three, preferred_element_type=jnp.float32)
    dx_rows = (jnp.einsum('secf,edf->secd', grad_one, w_one, preferred_element_type=jnp.float32) + jnp.einsum('secf,edf->secd', grad_three, w_three, preferred_element_type=jnp.float32)).astype(jnp.bfloat16)
    return dx_rows, wgrad_one, wgrad_three, wgrad_two


def solution(mesh):
    group_size = mesh.shape['ep']
    row_spec = P('ep', None)
    expert_spec = P('ep', None, None)
    copy_spec = P()

    def local_step(hidden, grad_out, routes, w_router, w_one, w_three, w_two, shared_one, shared_three, shared_two):
        tok_count, d_model = hidden.shape
        top_k = routes.shape[1]
        num_experts = w_router.shape[1]
        local_experts = w_one.shape[0]
        capacity = (5 * tok_count * top_k + 4 * num_experts - 1) // (4 * num_experts)
        buffer_shape = (group_size, local_experts, capacity, d_model)
        flat_shape = (num_experts * capacity, d_model)
        picked, pick_sum, weights = router_weights(hidden, routes, w_router)
        slot_ids, slot_token, slot_weight = slot_tables(routes, weights, num_experts, capacity)
        send_rows = jnp.take(hidden, slot_token, axis=0, mode='fill', fill_value=0).reshape(buffer_shape)
        recv_rows = lax.all_to_all(send_rows, 'ep', 0, 0)
        expert_out, expert_saved = expert_forward(recv_rows, w_one, w_three, w_two)
        back_rows = lax.all_to_all(expert_out, 'ep', 0, 0).reshape(flat_shape)
        gathered = jnp.take(back_rows, slot_ids, axis=0, mode='fill', fill_value=0)
        routed = jnp.sum(weights[:, :, None] * gathered, axis=1)
        shared_out, shared_saved = shared_forward(hidden, shared_one, shared_three, shared_two)
        hidden_out = (hidden.astype(jnp.float32) + shared_out + routed).astype(jnp.bfloat16)
        grad_rows = jnp.take(grad_out, slot_token, axis=0, mode='fill', fill_value=0)
        grad_send = (slot_weight[:, None] * grad_rows).astype(jnp.bfloat16).reshape(buffer_shape)
        grad_recv = lax.all_to_all(grad_send, 'ep', 0, 0)
        dx_rows, wgrad_one, wgrad_three, wgrad_two = expert_backward(recv_rows, grad_recv, expert_saved, w_one, w_three, w_two)
        dx_back = lax.all_to_all(dx_rows, 'ep', 0, 0).reshape(flat_shape)
        dx_routed = jnp.sum(jnp.take(dx_back, slot_ids, axis=0, mode='fill', fill_value=0), axis=1, dtype=jnp.float32)
        shared_dx, sgrad_one, sgrad_three, sgrad_two = shared_backward(hidden, grad_out, shared_saved, shared_one, shared_three, shared_two)
        route_dot = jnp.einsum('td,tkd->tk', grad_out, gathered, preferred_element_type=jnp.float32)
        grad_logits = router_grad_logits(route_dot, picked, pick_sum, weights, routes, num_experts)
        router_part = jnp.einsum('td,te->de', hidden, grad_logits, preferred_element_type=jnp.float32)
        gate_dx = jnp.einsum('te,de->td', grad_logits, w_router, preferred_element_type=jnp.float32)
        grad_hidden = (grad_out.astype(jnp.float32) + shared_dx + gate_dx + dx_routed).astype(jnp.bfloat16)
        grad_router = lax.psum(router_part, 'ep')
        grad_shared_one = lax.psum(sgrad_one, 'ep')
        grad_shared_three = lax.psum(sgrad_three, 'ep')
        grad_shared_two = lax.psum(sgrad_two, 'ep')
        return (hidden_out, grad_hidden, grad_router, wgrad_one.astype(jnp.bfloat16), wgrad_three.astype(jnp.bfloat16), wgrad_two.astype(jnp.bfloat16), grad_shared_one, grad_shared_three, grad_shared_two)

    return jax.shard_map(local_step, mesh=mesh, in_specs=(row_spec, row_spec, row_spec, copy_spec, expert_spec, expert_spec, expert_spec, copy_spec, copy_spec, copy_spec), out_specs=(row_spec, row_spec, copy_spec, expert_spec, expert_spec, expert_spec, copy_spec, copy_spec, copy_spec), check_vma=False)
```

profile of v0, /device:TPU:0, one launch (start us, length us, event | category | flops | bytes accessed | tf_op | source)
XLA Modules:
  0.0 4346.0 jit_solution(1446754647465012315)
XLA Ops:
  11.2 34.8 reduce-window.6
  45.9 2.0 slice.20
  48.0 1.5 copy.110
  50.9 2.1 fusion.43
  52.9 1.3 copy.82
  54.3 1.9 reshape.169
  56.2 225.3 %gather_fusion.1 = s32[12288]{0:T(1024)S(1)} fusion(s32[2048,64]{0,1:T(8,128)} %fusion.43, s32[12288]{0:T(1024)S(1)} %reshape.169), kind=kCustom, calls=%fused_computation.5 | custom fusion | bytes 196608 | tf_op jit(solution)/shard_map/jit(take_along_axis)/gather | solution.py:26
  281.5 2.0 reshape.178
  283.5 1.5 copy.87
  287.0 2.0 reshape.131
  290.2 1.9 reshape.185
  292.1 45.4 %scatter_custom_fusion = s32[15360]{0:T(1024)S(1)} fusion(s32[12288]{0:T(1024)S(1)} %bitcast.160, s32[12288]{0:T(1024)S(1)} %reshape.185, s32[]{:T(128)} %constant.43.clone.1), kind=kCustom, calls=%fused_computation.100 | custom fusion | bytes 61444 | tf_op jit(solution)/shard_map/scatter | solution.py:30
  337.6 95.1 %gather_fusion.2 = bf16[15360,1536]{1,0:T(8,128)(2,1)} fusion(bf16[2048,1536]{1,0:T(8,128)(2,1)} %param.14, s32[15360]{0:T(1024)S(1)} %fusion.50), kind=kCustom, calls=%fused_computation.clone | custom fusion | bytes 94433280 | tf_op jit(solution)/shard_map/jit(_take)/gather | solution.py:99
  432.7 31.8 broadcast_select_fusion.1
  464.5 521.5 %all_to_all.20 = bf16[16,4,240,1536]{3,2,1,0:T(8,128)(2,1)} all-to-all(bf16[16,4,240,1536]{3,2,1,0:T(8,128)(2,1)} %bitcast.154), channel_id=1, replica_groups=mesh['ep'=16] {'ep'}, dimensions={0} | all-to-all | bytes 94371840 | tf_op jit(solution)/shard_map/all_to_all | solution.py:100
  986.0 35.6 fusion.7
  1021.6 48.6 %fusion.14 = (bf16[16,4,240,512]{3,2,0,1:T(8,128)(2,1)}, f32[4,16,240,512]{3,2,1,0:T(8,128)}) fusion(f32[4,16,240,512]{3,2,1,0:T(8,128)} %fusion.7, bf16[4,1536,512]{2,1,0:T(8,128)(2,1)} %param.19, bf16[16,4,240,1536]{3,2,1,0:T(8,128)(2,1)} %all_to_all.20), kind=kOutput, calls=%fused_computation.32 | convolution fusion | flops 24206376960 | bytes 132120576 | tf_op jit(solution)/shard_map/secd,edf->secf/dot_general | solution.py:64
  1070.2 32.7 fusion.9
  1103.0 31.5 copy.92
  1134.5 9.9 all-to-all-start.1
  1144.4 5.6 fusion.42
  1150.0 232.7 %gather_fusion = f32[12288]{0:T(1024)S(1)} fusion(f32[2048,64]{0,1:T(8,128)} %fusion.42, s32[12288]{0:T(1024)S(1)} %copy-done.3), kind=kCustom, calls=%fused_computation.4 | custom fusion | bytes 196608 | tf_op jit(solution)/shard_map/jit(take_along_axis)/gather | solution.py:16
  1382.7 2.0 reshape.172
  1384.7 1.5 copy.83
  1387.4 1.3 copy.93
  1388.7 1.9 reshape.210
  1390.6 95.0 %gather_fusion.4 = bf16[15360,1536]{1,0:T(8,128)(2,1)} fusion(bf16[2048,1536]{1,0:T(8,128)(2,1)} %param.15, s32[15360]{0:T(1024)S(1)} %copy-done.21), kind=kCustom, calls=%fused_computation.2.clone | custom fusion | bytes 94433280 | tf_op jit(solution)/shard_map/jit(_take)/gather | solution.py:107
  1486.3 220.1 %all-to-all-done.1 = bf16[16,4,240,1536]{3,2,1,0:T(8,128)(2,1)} async-done(((bf16[16,4,240,1536]{3,2,1,0:T(8,128)(2,1)}), bf16[16,4,240,1536]{3,2,1,0:T(8,128)(2,1)}, u32[]{:S(2)}, u32[]{:S(2)}) %all-to-all-start.1) | async-done | bytes 47185952 | tf_op jit(solution)/shard_map/all_to_all | solution.py:102
  1706.5 355.1 %gather_fusion.3 = bf16[12288,1536]{1,0:T(8,128)(2,1)} fusion(bf16[15360,1536]{1,0:T(8,128)(2,1)} %bitcast.16, s32[12288]{0:T(1024)S(1)} %broadcast_clamp_fusion), kind=kCustom, calls=%fused_computation.1.clone | custom fusion | bytes 75546624 | tf_op jit(solution)/shard_map/jit(_take)/gather | solution.py:103
  2061.5 57.0 %reshape.213 = bf16[2048,6,1536]{2,1,0:T(8,128)(2,1)} reshape(bf16[12288,1536]{1,0:T(8,128)(2,1)} %gather_fusion.3) | data formatting | bytes 75497472 | tf_op jit(solution)/shard_map/jit(_take)/gather | solution.py:103
  2118.5 42.2 fusion
  2160.7 2.3 copy.108
  2163.0 1.4 fusion.46
  2165.7 1.9 reshape.193
  2167.6 45.8 %scatter_custom_fusion.1 = f32[15360]{0:T(1024)S(1)} fusion(s32[12288]{0:T(1024)} %bitcast.161, f32[12288]{0:T(1024)S(1)} %reshape.193, f32[]{:T(128)} %constant.42.clone.1), kind=kCustom, calls=%fused_computation.98 | custom fusion | bytes 61952 | tf_op jit(solution)/shard_map/scatter | solution.py:31
  2213.4 32.0 multiply_convert_fusion
  2245.4 519.2 %all_to_all.21 = bf16[16,4,240,1536]{3,2,1,0:T(8,128)(2,1)} all-to-all(bf16[16,4,240,1536]{3,2,1,0:T(8,128)(2,1)} %bitcast.153), channel_id=1, replica_groups=mesh['ep'=16] {'ep'}, dimensions={0} | all-to-all | bytes 94371840 | tf_op jit(solution)/shard_map/all_to_all | solution.py:109
  2764.7 55.2 %fusion.13 = (bf16[16,4,240,512]{3,2,0,1:T(8,128)(2,1)}, bf16[16,4,240,512]{3,2,0,1:T(8,128)(2,1)}) fusion(f32[4,16,240,512]{3,2,1,0:T(8,128)} %fusion.7, f32[4,16,240,512]{3,2,1,0:T(8,128)} %get-tuple-element.73, bf16[4,512,1536]{2,1,0:T(8,128)(2,1)} %param.20, bf16[16,4,240,1536]{3,2,1,0:T(8,128)(2,1)} %all_to_all.21), kind=kOutput, calls=%fused_computation.30 | convolution fusion | flops 24261427200 | bytes 147849216 | tf_op jit(solution)/shard_map/secd,efd->secf/dot_general | solution.py:73
  2819.9 42.3 fusion.35
  2862.2 54.2 %fusion.10 = bf16[16,4,240,1536]{3,2,0,1:T(8,128)(2,1)} fusion(f32[4,16,240,1536]{3,2,1,0:T(8,128)} %fusion.35, bf16[16,4,240,512]{3,2,0,1:T(8,128)(2,1)} %get-tuple-element.67, bf16[4,1536,512]{2,1,0:T(8,128)(2,1)} %param.19), kind=kOutput, calls=%fused_computation.25 | convolution fusion | flops 24206376960 | bytes 163577856 | tf_op jit(solution)/shard_map/secf,edf->secd/dot_general | solution.py:79
  2916.4 31.5 copy.97
  2947.9 8.6 all-to-all-start.3
  2956.8 11.8 fusion.57
  2968.6 10.8 fusion.58
  2979.4 18.6 multiply_convert_fusion.1
  2998.0 12.5 convolution_bitcast_fusion
  3010.5 10.8 convolution_bitcast_fusion.1
  3021.4 8.8 fusion.61
  3031.4 1.9 convolution_bitcast_fusion.2
  3033.3 12.7 fusion.59
  3046.0 9.5 fusion.60
  3055.5 660.9 %all-reduce.3.cloned.1.call-done = (f32[1536,64]{0,1:T(8,128)}, f32[1536,1024]{0,1:T(8,128)}, f32[1536,1024]{0,1:T(8,128)}, f32[1024,1536]{1,0:T(8,128)}) async-done(((f32[1536,64]{0,1:T(8,128)}, f32[1536,1024]{0,1:T(8,128)}, f32[1536,1024]{0,1:T(8,128)}, f32[1024,1536]{1,0:T(8,128)}), (f32[1536,64]{0,1:T(8,128)}, f32[1536,1024]{0,1:T(8,128)}, f32[1536,1024]{0,1:T(8,128)}, ...) | async-done | bytes 19267600 | tf_op jit(solution)/shard_map/psum | solution.py:119
  3716.4 6.6 copy.102
  3723.0 6.6 copy.103
  3729.5 34.2 bitcast_convert_fusion.1
  3763.8 34.3 bitcast_convert_fusion.2
  3798.1 32.1 bitcast_convert_fusion
  3830.2 300.4 %gather_fusion.5 = bf16[12288,1536]{1,0:T(8,128)(2,1)} fusion(bf16[15360,1536]{1,0:T(8,128)(2,1)} %bitcast.25, s32[12288]{0:T(1024)S(1)} %copy-done.5), kind=kCustom, calls=%fused_computation.3.clone | custom fusion | bytes 75546624 | tf_op jit(solution)/shard_map/jit(_take)/gather | solution.py:112
  4130.5 57.2 %reshape.219 = bf16[2048,6,1536]{2,1,0:T(8,128)(2,1)} reshape(bf16[12288,1536]{1,0:T(8,128)(2,1)} %gather_fusion.5) | data formatting | bytes 75497472 | tf_op jit(solution)/shard_map/jit(_take)/gather | solution.py:112
  4187.7 112.4 %convert_reduce_fusion = (f32[2048,1536]{1,0:T(8,128)}, f32[2048,1536]{1,0:T(8,128)}) fusion(bf16[2048,6,1536]{2,1,0:T(8,128)(2,1)} %reshape.219, pred[2048,6]{1,0:T(8,128)(4,1)S(1)} %copy-done.10, bf16[2048,6,1536]{2,1,0:T(8,128)(2,1)} %reshape.213, f32[2048,6]{1,0:T(8,128)} %copy.84), kind=kLoop, calls=%fused_computation.8 | loop fusion | flops 125829120 | bytes 100724736 | tf_op jit(solution)/shard_map/reduce_sum | solution.py:112
  4300.1 13.1 add_convert_fusion.2
  4313.3 17.8 add_convert_fusion.1
  4331.0 1.8 copy.142
  4332.8 5.9 copy.143
  (106 shorter events, 13.2 us)
Async XLA Ops:
  7.2 2972.2 %copy-start = (bf16[1024,1536]{1,0:T(8,128)(2,1)S(1)}, bf16[1024,1536]{1,0:T(8,128)(2,1)}, u32[]{:S(2)}) copy-start(bf16[1024,1536]{1,0:T(8,128)(2,1)} %param.23) | copy-start | bytes 9437188
  9.5 0.8 copy-start.6
  56.2 225.3 %copy-start.2 = (s32[12288]{0:T(1024)}, s32[12288]{0:T(1024)S(1)}, u32[]{:S(2)}) copy-start(s32[12288]{0:T(1024)S(1)} %reshape.169) | copy-start | bytes 147460
  56.2 228.8 %copy-start.14 = (s32[2048,6]{0,1:T(8,128)S(1)}, s32[2048,6]{0,1:T(8,128)}, u32[]{:S(2)}) copy-start(s32[2048,6]{0,1:T(8,128)} %param.16) | copy-start | bytes 147460
  285.7 147.0 %copy-start.18 = (s32[2048,6]{0,1:T(8,128)}, s32[2048,6]{0,1:T(8,128)S(1)}, u32[]{:S(2)}) copy-start(s32[2048,6]{0,1:T(8,128)S(1)} %get-tuple-element.65) | copy-start | bytes 147460
  289.1 3.0 copy-start.30
  337.6 95.1 %copy-start.26 = (pred[15360]{0:T(1024)(128)(4,1)}, pred[15360]{0:T(1024)(128)(4,1)S(1)}, u32[]{:S(2)}) copy-start(pred[15360]{0:T(1024)(128)(4,1)S(1)} %compare_and_fusion.2) | copy-start | bytes 46084
  337.6 95.1 %copy-start.20 = (s32[15360]{0:T(1024)}, s32[15360]{0:T(1024)S(1)}, u32[]{:S(2)}) copy-start(s32[15360]{0:T(1024)S(1)} %fusion.50) | copy-start | bytes 184324
  1134.5 9.9 copy-start.25
  1134.5 572.0 %all-to-all-start.1 = ((bf16[16,4,240,1536]{3,2,1,0:T(8,128)(2,1)}), bf16[16,4,240,1536]{3,2,1,0:T(8,128)(2,1)}, u32[]{:S(2)}, u32[]{:S(2)}) async-start(bf16[16,4,240,1536]{3,2,1,0:T(8,128)(2,1)} %copy.92), calls=%async_computation.1 | async-start | bytes 94371840 | tf_op jit(solution)/shard_map/all_to_all | solution.py:102
  1144.4 5.6 copy-start.3
  1150.0 236.3 %copy-start.29 = (pred[2048,6]{0,1:T(8,128)(4,1)S(1)}, pred[2048,6]{0,1:T(8,128)(4,1)}, u32[]{:S(2)}) copy-start(pred[2048,6]{0,1:T(8,128)(4,1)} %get-tuple-element.64) | copy-start | bytes 36868
  1150.0 237.4 %copy-start.19 = (s32[2048,6]{0,1:T(8,128)S(1)}, s32[2048,6]{0,1:T(8,128)}, u32[]{:S(2)}) copy-start(s32[2048,6]{0,1:T(8,128)} %copy-done.18) | copy-start | bytes 147460
  1150.0 240.6 %copy-start.21 = (s32[15360]{0:T(1024)S(1)}, s32[15360]{0:T(1024)}, u32[]{:S(2)}) copy-start(s32[15360]{0:T(1024)} %copy-done.20) | copy-start | bytes 184324
  1386.3 99.4 %copy-start.11 = (f32[2048,6]{0,1:T(8,128)}, f32[2048,6]{0,1:T(8,128)S(1)}, u32[]{:S(2)}) copy-start(f32[2048,6]{0,1:T(8,128)S(1)} %copy.83) | copy-start | bytes 147460
  1390.6 95.0 %copy-start.22 = (pred[2048,6]{0,1:T(8,128)(4,1)S(1)}, pred[2048,6]{0,1:T(8,128)(4,1)}, u32[]{:S(2)}) copy-start(pred[2048,6]{0,1:T(8,128)(4,1)} %get-tuple-element.66) | copy-start | bytes 36868
  1486.3 575.2 %copy-start.4 = (s32[12288]{0:T(1024)}, s32[12288]{0:T(1024)S(1)}, u32[]{:S(2)}) copy-start(s32[12288]{0:T(1024)S(1)} %broadcast_clamp_fusion) | copy-start | bytes 147460
  2061.5 57.0 %copy-start.9 = (pred[2048,6]{1,0:T(8,128)(4,1)S(1)}, pred[2048,6]{1,0:T(8,128)(4,1)}, u32[]{:S(2)}) copy-start(pred[2048,6]{1,0:T(8,128)(4,1)} %copy.88) | copy-start | bytes 36868
  2118.5 44.5 %copy-start.12 = (f32[2048,6]{0,1:T(8,128)S(1)}, f32[2048,6]{0,1:T(8,128)}, u32[]{:S(2)}) copy-start(f32[2048,6]{0,1:T(8,128)} %copy-done.11) | copy-start | bytes 147460
  2118.5 44.5 %copy-start.23 = (pred[2048,6]{0,1:T(8,128)(4,1)S(1)}, pred[2048,6]{0,1:T(8,128)(4,1)}, u32[]{:S(2)}) copy-start(pred[2048,6]{0,1:T(8,128)(4,1)} %get-tuple-element.66) | copy-start | bytes 36868
  2118.5 94.9 %copy-start.27 = (pred[15360]{0:T(1024)(128)(4,1)S(1)}, pred[15360]{0:T(1024)(128)(4,1)}, u32[]{:S(2)}) copy-start(pred[15360]{0:T(1024)(128)(4,1)} %copy-done.26) | copy-start | bytes 46084
  2163.0 82.5 %copy-start.16 = (f32[2048,1,6]{0,2,1:T(8,128)}, f32[2048,1,6]{0,2,1:T(8,128)S(1)}, u32[]{:S(2)}) copy-start(f32[2048,1,6]{0,2,1:T(8,128)S(1)} %copy.108) | copy-start | bytes 147460
  2947.9 882.2 %all-to-all-start.3 = ((bf16[16,4,240,1536]{3,2,1,0:T(8,128)(2,1)}), bf16[16,4,240,1536]{3,2,1,0:T(8,128)(2,1)}, u32[]{:S(2)}, u32[]{:S(2)}) async-start(bf16[16,4,240,1536]{3,2,1,0:T(8,128)(2,1)} %copy.97), calls=%async_computation.3 | async-start | bytes 94371840 | tf_op jit(solution)/shard_map/all_to_all | solution.py:111
  2956.5 759.9 %all-reduce.3.cloned.1.call-start = ((), (), s32[]{:S(2)}) async-start(), calls=%async_computation.4 | async-start | bytes 38535168 | tf_op jit(solution)/shard_map/psum | solution.py:119
  2956.8 11.8 copy-start.32
  2998.0 12.5 copy-start.36
  2998.0 23.3 slice-start.2
  3010.5 10.8 slice-start.3
  3010.5 10.8 copy-start.34
  3010.5 20.9 slice-start
  3021.3 8.9 copy-start.28
  3021.3 8.9 copy-start.31
  3021.3 8.9 copy-start.13
  3021.3 8.9 copy-start.17
  3021.3 8.9 copy-start.24
  3021.3 8.9 copy-start.15
  3021.3 10.0 slice-start.1
  3030.6 0.7 copy-start.7
  3033.3 12.7 copy-start.33
  3033.3 12.7 copy-start.35
  3798.1 32.1 copy-start.5
  4130.5 57.2 %copy-start.10 = (pred[2048,6]{1,0:T(8,128)(4,1)S(1)}, pred[2048,6]{1,0:T(8,128)(4,1)}, u32[]{:S(2)}) copy-start(pred[2048,6]{1,0:T(8,128)(4,1)} %copy.88) | copy-start | bytes 36868
  4187.7 112.4 %copy-start.1 = (bf16[2048,1536]{1,0:T(8,128)(2,1)S(1)}, bf16[2048,1536]{1,0:T(8,128)(2,1)}, u32[]{:S(2)}) copy-start(bf16[2048,1536]{1,0:T(8,128)(2,1)} %param.14) | copy-start | bytes 18874372
  4300.1 13.1 copy-start.8
Sparse Core Ops, SparseCore 0:
  3033.4 682.9 all-reduce.2
where the time goes:
time: 4400 us; the launch traced here: 4350 us
  local copies, waits for them, and re-layouts  1630 us (37%)
  blocking collectives  1040 us (24%)
  waiting for transfers between devices  881 us (20%)
  matrix products  545 us (12%)
  other arithmetic  220 us (5%)
    psum x1, waiting for transfers between devices, local_step(): grad_router = lax.psum(router_part, 'ep')  661 us
    all_to_all x1, blocking collectives, local_step(): recv_rows = lax.all_to_all(send_rows, 'ep', 0, 0)  522 us
    all_to_all x1, blocking collectives, local_step(): grad_recv = lax.all_to_all(grad_send, 'ep', 0, 0)  519 us
    gather x2, local copies, waits for them, and re-layouts, local_step(): gathered = jnp.take(back_rows, slot_ids, axis=0, mode='fill', fill_value=0)  412 us
    gather x2, local copies, waits for them, and re-layouts, local_step(): jnp.take(dx_back, slot_ids, axis=0, mode='fill', fill_value=0)  358 us
    gather x5, local copies, waits for them, and re-layouts, router_weights(): picked = jnp.take_along_axis(jax.nn.sigmoid(logits), routes, axis=1)  239 us
    gather x3, local copies, waits for them, and re-layouts, slot_tables(): position = jnp.take_along_axis(before, routes, axis=1)  229 us
    all_to_all x1, waiting for transfers between devices, local_step(): back_rows = lax.all_to_all(expert_out, 'ep', 0, 0).reshape(flat_shape)  220 us
  transfers between devices with their start and end apart: 3, of which 2 were waited for; matrix products, arithmetic and copies ran while one was open for 13% of the time, Pallas kernels for 0%

commit v1 on v0

v1 whole, which is shorter than its diff:
```python
import functools

import jax
import jax.numpy as jnp
from jax import lax
from jax.experimental import pallas as pl
from jax.experimental.pallas import tpu as pltpu
from jax.sharding import PartitionSpec as P


ROUTE_SCALE = 2.5
LANES = 128
UNROLL = 8
CHOICE_STRIDE = 8
SPARE_ROWS = 32
VMEM_BYTES = 60 * 2 ** 20


def spread(dst, block, first_row):
    rows, width = block.shape
    chunks = width // LANES
    for c in range(chunks):
        dst[pl.ds(first_row * chunks + c, rows, stride=chunks), :] = block[:, c * LANES:(c + 1) * LANES].astype(jnp.float32)


def gather_kernel(near_experts, num_experts, capacity, weighted, *refs):
    if weighted:
        token_ref, count_ref, weight_ref, table_ref, near_ref, far_ref, table, rows = refs
    else:
        token_ref, count_ref, table_ref, near_ref, far_ref, table, rows = refs
    source, expert = pl.program_id(0), pl.program_id(1)
    tok_count, width = table_ref.shape
    chunks = width // LANES
    slot = source * num_experts + expert

    @pl.when(expert == 0)
    def _():
        @pl.loop(0, tok_count // LANES)
        def _(i):
            first = pl.multiple_of(i * LANES, LANES)
            spread(table, table_ref[pl.ds(first, LANES), :], first)

        table[pl.ds(tok_count * chunks, chunks), :] = jnp.zeros((chunks, LANES), jnp.float32)

    steps = (count_ref[slot] + (UNROLL - 1)) // UNROLL

    @pl.loop(0, steps)
    def _(i):
        for u in range(UNROLL):
            place = i * UNROLL + u
            token = token_ref[slot * capacity + place]
            row = table[pl.ds(token * chunks, chunks), :]
            if weighted:
                row = row * weight_ref[slot * capacity + place]
            rows[pl.ds(place * chunks, chunks), :] = row

    @pl.loop(steps, capacity // UNROLL)
    def _(i):
        rows[pl.ds(pl.multiple_of(i * UNROLL * chunks, UNROLL), UNROLL * chunks), :] = jnp.zeros((UNROLL * chunks, LANES), jnp.float32)

    def store(out_ref):
        for c in range(chunks):
            out_ref[:, c * LANES:(c + 1) * LANES] = rows[pl.ds(c, capacity, stride=chunks), :].astype(out_ref.dtype)

    @pl.when(expert < near_experts)
    def _():
        store(near_ref)

    @pl.when(expert >= near_experts)
    def _():
        store(far_ref)


def gather_rows(table, slot_token, counts, weights, near_experts, num_experts, capacity):
    num_sources = counts.shape[0] // num_experts
    tok_count, width = table.shape[0] // num_sources, table.shape[1]
    chunks = width // LANES
    scalars = [slot_token, counts] + ([] if weights is None else [weights])
    out_block = (None, None, capacity, width)
    far_experts = num_experts - near_experts
    return pl.pallas_call(
        functools.partial(gather_kernel, near_experts, num_experts, capacity, weights is not None),
        grid_spec=pltpu.PrefetchScalarGridSpec(
            num_scalar_prefetch=len(scalars),
            grid=(num_sources, num_experts),
            in_specs=[pl.BlockSpec((tok_count, width), lambda s, e, *_: (s, 0))],
            out_specs=[
                pl.BlockSpec(out_block, lambda s, e, *_: (jnp.minimum(e, near_experts - 1), s, 0, 0)),
                pl.BlockSpec(out_block, lambda s, e, *_: (jnp.maximum(e - near_experts, 0), s, 0, 0)),
            ],
            scratch_shapes=[pltpu.VMEM(((tok_count + 8) * chunks, LANES), jnp.float32), pltpu.VMEM((capacity * chunks, LANES), jnp.float32)],
        ),
        out_shape=[jax.ShapeDtypeStruct((n, num_sources, capacity, width), table.dtype) for n in (near_experts, far_experts)],
        compiler_params=pltpu.CompilerParams(vmem_limit_bytes=VMEM_BYTES),
        cost_estimate=pl.CostEstimate(flops=2 * 10 ** 10, bytes_accessed=10 ** 8, transcendentals=0),
        name='gather_rows',
    )(*scalars, table)


def combine_kernel(num_blocks, capacity, with_dots, *refs):
    if with_dots:
        code_ref, count_ref, weight_ref, block_ref, base_ref, grad_ref, out_ref, dots_ref, total, rows, grads, dots = refs
    else:
        code_ref, count_ref, block_ref, base_ref, out_ref, total, rows = refs
    step = pl.program_id(0)
    width = block_ref.shape[-1]
    chunks = width // LANES
    tok_count = total.shape[0] // chunks - SPARE_ROWS

    def clear(ref):
        @pl.loop(0, ref.shape[0] // LANES)
        def _(i):
            ref[pl.ds(pl.multiple_of(i * LANES, LANES), LANES), :] = jnp.zeros((LANES, LANES), jnp.float32)

    @pl.when(step == 0)
    def _():
        clear(total)
        if with_dots:
            clear(dots)

            @pl.loop(0, tok_count // LANES)
            def _(i):
                first = pl.multiple_of(i * LANES, LANES)
                spread(grads, grad_ref[pl.ds(first, LANES), :], first)

    @pl.when(step < num_blocks)
    def _():
        spread(rows, block_ref[...], 0)
        steps = (count_ref[step] + (UNROLL - 1)) // UNROLL

        @pl.loop(0, steps)
        def _(i):
            stores = []
            for u in range(UNROLL):
                place = i * UNROLL + u
                code = code_ref[step * capacity + place]
                token_row = (code // CHOICE_STRIDE) * chunks
                row = rows[pl.ds(place * chunks, chunks), :]
                if with_dots:
                    dot = jnp.sum(row * grads[pl.ds(token_row, chunks), :], axis=0, keepdims=True)
                    stores.append((dots, pl.ds(code, 1), dot))
                    row = row * weight_ref[step * capacity + place]
                stores.append((total, pl.ds(token_row, chunks), total[pl.ds(token_row, chunks), :] + row))
            for ref, where, value in stores:
                ref[where, :] = value

    @pl.when(step >= num_blocks)
    def _():
        rows_out = out_ref.shape[0]
        first = (step - num_blocks) * rows_out
        for c in range(chunks):
            part = total[pl.ds(first * chunks + c, rows_out, stride=chunks), :]
            out_ref[:, c * LANES:(c + 1) * LANES] = (base_ref[:, c * LANES:(c + 1) * LANES] + part).astype(out_ref.dtype)
        if with_dots:
            dots_ref[...] = dots[pl.ds(pl.multiple_of(first * CHOICE_STRIDE, LANES), rows_out * CHOICE_STRIDE), :]


def combine_rows(landed, slot_code, counts, base, weights=None, grads=None):
    num_blocks, capacity, width = landed.shape
    tok_count = base.shape[0]
    chunks = width // LANES
    out_rows = LANES
    with_dots = weights is not None
    last = num_blocks - 1
    padded = tok_count + SPARE_ROWS
    out_spec = pl.BlockSpec((out_rows, width), lambda i, *_: (jnp.maximum(i - num_blocks, 0), 0))
    in_specs = [pl.BlockSpec((None, capacity, width), lambda i, *_: (jnp.minimum(i, last), 0, 0)), out_spec]
    out_specs, out_shape = [out_spec], [jax.ShapeDtypeStruct((tok_count, width), landed.dtype)]
    scratch = [pltpu.VMEM((padded * chunks, LANES), jnp.float32), pltpu.VMEM((capacity * chunks, LANES), jnp.float32)]
    scalars, arrays = [slot_code, counts], [landed, base]
    if with_dots:
        scalars.append(weights)
        arrays.append(grads)
        in_specs.append(pl.BlockSpec((tok_count, width), lambda i, *_: (0, 0)))
        out_specs.append(pl.BlockSpec((out_rows * CHOICE_STRIDE, LANES), lambda i, *_: (jnp.maximum(i - num_blocks, 0), 0)))
        out_shape.append(jax.ShapeDtypeStruct((tok_count * CHOICE_STRIDE, LANES), jnp.float32))
        scratch += [pltpu.VMEM((padded * chunks, LANES), jnp.float32), pltpu.VMEM((padded * CHOICE_STRIDE, LANES), jnp.float32)]
    return pl.pallas_call(
        functools.partial(combine_kernel, num_blocks, capacity, with_dots),
        grid_spec=pltpu.PrefetchScalarGridSpec(
            num_scalar_prefetch=len(scalars),
            grid=(num_blocks + tok_count // out_rows,),
            in_specs=in_specs,
            out_specs=out_specs,
            scratch_shapes=scratch,
        ),
        out_shape=out_shape,
        compiler_params=pltpu.CompilerParams(vmem_limit_bytes=VMEM_BYTES),
        cost_estimate=pl.CostEstimate(flops=2 * 10 ** 10, bytes_accessed=10 ** 8, transcendentals=0),
        name='combine_dots' if with_dots else 'combine_rows',
    )(*scalars, *arrays)


def silu_parts(pre_act):
    sig_val = jax.nn.sigmoid(pre_act)
    return pre_act * sig_val, sig_val * (1.0 + pre_act * (1.0 - sig_val))


def router_tables(hidden, routes, w_router, capacity):
    tok_count, num_experts = hidden.shape[0], w_router.shape[1]
    scores = jax.nn.sigmoid(jnp.dot(hidden, w_router, preferred_element_type=jnp.float32))
    is_choice = routes[:, :, None] == jnp.arange(num_experts, dtype=jnp.int32)
    picked = jnp.sum(jnp.where(is_choice, scores[:, None, :], 0.0), axis=2)
    pick_sum = jnp.sum(picked, axis=1, keepdims=True)
    weights = ROUTE_SCALE * picked / pick_sum
    chosen = jnp.any(is_choice, axis=1)
    choice_map = jnp.sum(jnp.where(is_choice, jnp.arange(routes.shape[1], dtype=jnp.int32)[None, :, None], 0), axis=1)
    weight_map = ROUTE_SCALE * scores / pick_sum
    row_ids = lax.broadcasted_iota(jnp.int32, (tok_count, tok_count), 0)
    col_ids = lax.broadcasted_iota(jnp.int32, (tok_count, tok_count), 1)
    earlier = (col_ids < row_ids).astype(jnp.bfloat16)
    before = jnp.dot(earlier, chosen.astype(jnp.bfloat16), preferred_element_type=jnp.float32).astype(jnp.int32)
    position_map = jnp.where(chosen, before, -1).T
    code_map = (choice_map + CHOICE_STRIDE * jnp.arange(tok_count, dtype=jnp.int32)[:, None]).T
    hit = position_map[:, None, :] == jnp.arange(capacity, dtype=jnp.int32)[None, :, None]
    slot_code = jnp.sum(jnp.where(hit, code_map[:, None, :], 0), axis=2)
    slot_weight = jnp.sum(jnp.where(hit, weight_map.T[:, None, :], 0.0), axis=2)
    counts = jnp.minimum(jnp.sum(chosen.astype(jnp.int32), axis=0), capacity)
    empty = jnp.arange(capacity, dtype=jnp.int32)[None, :] >= counts[:, None]
    slot_code = jnp.where(empty, CHOICE_STRIDE * tok_count, slot_code)
    return picked, pick_sum, weights, slot_code, slot_weight, counts


def router_grad_logits(route_dot, picked, pick_sum, weights, routes, num_experts):
    mean_term = jnp.sum(route_dot * weights, axis=1, keepdims=True) / ROUTE_SCALE
    grad_pick = ROUTE_SCALE / pick_sum * (route_dot - mean_term) * picked * (1.0 - picked)
    is_choice = routes[:, :, None] == jnp.arange(num_experts, dtype=jnp.int32)
    return jnp.sum(jnp.where(is_choice, grad_pick[:, :, None], 0.0), axis=1).astype(jnp.bfloat16)


def shared_forward(hidden, shared_one, shared_three, shared_two):
    pre_one = jnp.dot(hidden, shared_one, preferred_element_type=jnp.float32)
    pre_three = jnp.dot(hidden, shared_three, preferred_element_type=jnp.float32)
    act_one, dact_one = silu_parts(pre_one)
    mid_act = (act_one * pre_three).astype(jnp.bfloat16)
    return jnp.dot(mid_act, shared_two, preferred_element_type=jnp.float32), (pre_three, act_one, dact_one, mid_act)


def shared_backward(hidden, grad_out, saved_acts, shared_one, shared_three, shared_two):
    pre_three, act_one, dact_one, mid_act = saved_acts
    grad_mid = jnp.einsum('td,fd->tf', grad_out, shared_two, preferred_element_type=jnp.float32)
    grad_one = (grad_mid * pre_three * dact_one).astype(jnp.bfloat16)
    grad_three = (grad_mid * act_one).astype(jnp.bfloat16)
    wgrad_one = jnp.einsum('td,tf->df', hidden, grad_one, preferred_element_type=jnp.float32)
    wgrad_three = jnp.einsum('td,tf->df', hidden, grad_three, preferred_element_type=jnp.float32)
    wgrad_two = jnp.einsum('tf,td->fd', mid_act, grad_out, preferred_element_type=jnp.float32)
    dx_part = jnp.einsum('tf,df->td', grad_one, shared_one, preferred_element_type=jnp.float32) + jnp.einsum('tf,df->td', grad_three, shared_three, preferred_element_type=jnp.float32)
    return dx_part, wgrad_one, wgrad_three, wgrad_two


def expert_forward(in_rows, w_one, w_three, w_two):
    pre_one = jnp.einsum('erd,edf->erf', in_rows, w_one, preferred_element_type=jnp.float32)
    pre_three = jnp.einsum('erd,edf->erf', in_rows, w_three, preferred_element_type=jnp.float32)
    act_one, dact_one = silu_parts(pre_one)
    mid_act = (act_one * pre_three).astype(jnp.bfloat16)
    expert_out = jnp.einsum('erf,efd->erd', mid_act, w_two, preferred_element_type=jnp.float32).astype(jnp.bfloat16)
    return expert_out, (pre_three, act_one, dact_one, mid_act)


def expert_middle(in_rows, grad_rows, saved_acts, w_two, send):
    pre_three, act_one, dact_one, mid_act = saved_acts
    wgrad_two = jnp.einsum('erf,erd->efd', mid_act, grad_rows, preferred_element_type=jnp.float32)
    wgrad_two = send(wgrad_two)
    grad_mid = jnp.einsum('erd,efd->erf', grad_rows, w_two, preferred_element_type=jnp.float32)
    grad_one = (grad_mid * pre_three * dact_one).astype(jnp.bfloat16)
    grad_three = (grad_mid * act_one).astype(jnp.bfloat16)
    wgrad_one = jnp.einsum('erd,erf->edf', in_rows, grad_one, preferred_element_type=jnp.float32)
    wgrad_one = send(wgrad_one)
    wgrad_three = jnp.einsum('erd,erf->edf', in_rows, grad_three, preferred_element_type=jnp.float32)
    wgrad_three = send(wgrad_three)
    return grad_one, grad_three, (wgrad_one, wgrad_three, wgrad_two)


def expert_dx(grad_one, grad_three, w_one, w_three):
    return (jnp.einsum('erf,edf->erd', grad_one, w_one, preferred_element_type=jnp.float32) + jnp.einsum('erf,edf->erd', grad_three, w_three, preferred_element_type=jnp.float32)).astype(jnp.bfloat16)


def solution(mesh):
    group_size = mesh.shape['ep']
    row_spec = P('ep', None)
    expert_spec = P('ep', None, None)
    copy_spec = P()
    half_groups = [[i for i in range(group_size) if (i >> 1) & 1 == side] for side in (0, 1)]
    half_size = group_size // 2
    across = [(i, i ^ 2) for i in range(group_size)]

    def local_step(hidden, grad_out, routes, w_router, w_one, w_three, w_two, shared_one, shared_three, shared_two):
        tok_count, d_model = hidden.shape
        top_k = routes.shape[1]
        num_experts = w_router.shape[1]
        local_experts = w_one.shape[0]
        capacity = (5 * tok_count * top_k + 4 * num_experts - 1) // (4 * num_experts)
        side = (lax.axis_index('ep') // 2) % 2

        def swap(array):
            return lax.ppermute(array, 'ep', across)

        def gather_half(array):
            return lax.all_gather(array, 'ep', axis=0, tiled=True, axis_index_groups=half_groups)

        def exchange(array):
            return lax.all_to_all(array, 'ep', 0, 0, axis_index_groups=half_groups)

        def by_worker(table):
            table = table.reshape(group_size // 4, 2, 2, local_experts, -1).transpose(0, 2, 1, 3, 4)
            table = jnp.where(side == 1, table[:, :, ::-1], table)
            return table.reshape(half_size, 2, local_experts, -1)

        hidden_half = gather_half(hidden)
        grad_half = gather_half(grad_out)
        far_one, far_three, far_two = swap(w_one), swap(w_three), swap(w_two)

        picked, pick_sum, weights, slot_code, slot_weight, counts = router_tables(hidden, routes, w_router, capacity)
        slot_code, slot_weight, counts = by_worker(slot_code), by_worker(slot_weight), by_worker(counts)
        meta = jnp.concatenate([(slot_code // CHOICE_STRIDE).astype(jnp.float32), slot_weight, counts.astype(jnp.float32)], axis=3)
        meta = exchange(meta)
        row_token = meta[..., :capacity].astype(jnp.int32).reshape(-1)
        row_weight = meta[..., capacity:2 * capacity].reshape(-1)
        row_counts = meta[..., 2 * capacity].astype(jnp.int32).reshape(-1)
        slot_code, slot_weight, counts = slot_code.reshape(-1), slot_weight.reshape(-1), counts.reshape(-1)

        shared_out, shared_saved = shared_forward(hidden, shared_one, shared_three, shared_two)
        shared_dx, sgrad_one, sgrad_three, sgrad_two = shared_backward(hidden, grad_out, shared_saved, shared_one, shared_three, shared_two)
        out_base = hidden.astype(jnp.float32) + shared_out
        dx_base = grad_out.astype(jnp.float32) + shared_dx

        def expert_rows(table, tokens, scale):
            shape = (local_experts, half_size * capacity, d_model)
            near, far = gather_rows(table, tokens, row_counts, scale, local_experts, 2 * local_experts, capacity)
            return near.reshape(shape), far.reshape(shape)

        def pack(near_rows, far_rows):
            rows = jnp.stack([near_rows, far_rows]).reshape(2, local_experts, half_size, capacity, d_model)
            return rows.transpose(2, 0, 1, 3, 4)

        def send_back(packed):
            return exchange(packed).reshape(num_experts, capacity, d_model)

        sgrads = (sgrad_one, sgrad_three, sgrad_two)
        row_token, out_base, dx_base, sgrads = lax.optimization_barrier((row_token, out_base, dx_base, sgrads))
        near_in, far_in = expert_rows(hidden_half, row_token, None)
        near_out, near_saved = expert_forward(near_in, w_one, w_three, w_two)
        near_out, sgrads = lax.optimization_barrier((near_out, sgrads))
        shared_grads = lax.psum(sgrads, 'ep')
        far_out, far_saved = expert_forward(far_in, far_one, far_three, far_two)
        out_packed, row_token = lax.optimization_barrier((pack(near_out, far_out), row_token))
        out_landed = send_back(out_packed)

        near_grad, far_grad = expert_rows(grad_half, row_token, row_weight)
        far_u, far_v, back_wgrads = expert_middle(far_in, far_grad, far_saved, far_two, swap)
        near_u, near_v, near_wgrads = expert_middle(near_in, near_grad, near_saved, w_two, lambda array: array)
        near_dx, far_dx = expert_dx(near_u, near_v, w_one, w_three), expert_dx(far_u, far_v, far_one, far_three)
        dx_packed = pack(near_dx, far_dx)
        dx_landed = send_back(dx_packed)

        hidden_out, dots = combine_rows(out_landed, slot_code, counts, out_base, slot_weight, grad_out)
        route_dot = jnp.sum(dots, axis=1).reshape(tok_count, CHOICE_STRIDE)[:, :top_k]
        grad_logits = router_grad_logits(route_dot, picked, pick_sum, weights, routes, num_experts)
        router_part = jnp.einsum('td,te->de', hidden, grad_logits, preferred_element_type=jnp.float32)
        gate_dx = jnp.einsum('te,de->td', grad_logits, w_router, preferred_element_type=jnp.float32)
        grad_hidden, = combine_rows(dx_landed, slot_code, counts, dx_base + gate_dx)
        router_part, shared_grads = lax.optimization_barrier((router_part, shared_grads))
        grad_router = lax.psum(router_part, 'ep')
        grad_w_one, grad_w_three, grad_w_two = [(near + far).astype(jnp.bfloat16) for near, far in zip(near_wgrads, back_wgrads)]
        return (hidden_out, grad_hidden, grad_router, grad_w_one, grad_w_three, grad_w_two, *shared_grads)

    return jax.shard_map(local_step, mesh=mesh, in_specs=(row_spec, row_spec, row_spec, copy_spec, expert_spec, expert_spec, expert_spec, copy_spec, copy_spec, copy_spec), out_specs=(row_spec, row_spec, copy_spec, expert_spec, expert_spec, expert_spec, copy_spec, copy_spec, copy_spec), check_vma=False)
```

time: 4400 us -> 2350 us (0.53); the launches traced: 4350 us -> 2340 us
  local copies, waits for them, and re-layouts: 1630 us -> 29.2 us
  blocking collectives: 1040 us -> 0 us
  Pallas kernels: 0 us -> 404 us
  waiting for transfers between devices: 881 us -> 1180 us
  other arithmetic: 220 us -> 106 us
    gather x14 -> x0, local copies, waits for them, and re-layouts: 1430 us -> none  [the longest x2 412 us: local_step(): gathered = jnp.take(back_rows, slot_ids, axis=0, mode='fill', fill_value=0)]
    all_to_all x2 -> x0, blocking collectives: 1040 us -> none  [the longest x1 522 us: local_step(): recv_rows = lax.all_to_all(send_rows, 'ep', 0, 0)]
    ppermute x0 -> x6, waiting for transfers between devices: none -> 891 us  [swap(): return lax.ppermute(array, 'ep', across)]
    psum x1, waiting for transfers between devices: 661 us -> 0.01 us  [local_step(): grad_router = lax.psum(router_part, 'ep')]
    pallas_call x0 -> x4, Pallas kernels: none -> 404 us  [the longest x2 236 us: combine_rows(): pl.pallas_call(functools.partial(combine_kernel, num_blocks, capacity, wi...]
    scatter x2 -> x0, local copies, waits for them, and re-layouts: 91.2 us -> none  [the longest x1 45.8 us: slot_tables(): jnp.zeros((num_experts * capacity,), jnp.float32).at[flat_slots]]
    reduce_sum x3 -> x6, other arithmetic: 114 us -> 38 us  [the longest x1 15.9 us: router_tables(): slot_weight = jnp.sum(jnp.where(hit, weight_map.T[:, None, :], 0.0), axis=2)]
    all_gather x0 -> x2, waiting for transfers between devices: none -> 65.1 us  [gather_half(): lax.all_gather(array, 'ep', axis=0, tiled=True, axis_index_groups=half_gr...]
  transfers between devices with their start and end apart: 3 -> 13, of which waited for: 2 -> 6; matrix products, arithmetic and copies ran while one was open for 13% -> 30% of each run, Pallas kernels for 0% -> 17%
where the time goes in v1:
time: 2350 us; the launch traced here: 2340 us
  waiting for transfers between devices  1180 us (50%)
  matrix products  577 us (25%)
  Pallas kernels  404 us (17%)
  other arithmetic  106 us (5%)
  starting transfers between devices  29.6 us (1%)
  local copies, waits for them, and re-layouts  29.2 us (1%)
    ppermute x6, waiting for transfers between devices, swap(): return lax.ppermute(array, 'ep', across)  891 us
    pallas_call x2, Pallas kernels, combine_rows(): pl.pallas_call(functools.partial(combine_kernel, num_blocks, capacity, wi...  236 us
    all_to_all x3, waiting for transfers between devices, exchange(): return lax.all_to_all(array, 'ep', 0, 0, axis_index_groups=half_groups)  225 us
    pallas_call x2, Pallas kernels, gather_rows(): pl.pallas_call(functools.partial(gather_kernel, near_experts, num_experts...  168 us
    all_gather x2, waiting for transfers between devices, gather_half(): lax.all_gather(array, 'ep', axis=0, tiled=True, axis_index_groups=half_gr...  65.1 us
    transpose x2, other arithmetic, pack(): return rows.transpose(2, 0, 1, 3, 4)  63.7 us
    dot_general x2, matrix products, expert_middle(): jnp.einsum('erd,efd->erf', grad_rows, w_two, preferred_element_type=jnp.f...  59.3 us
    dot_general x2, matrix products, expert_forward(): jnp.einsum('erd,edf->erf', in_rows, w_three, preferred_element_type=jnp.f...  59.2 us
  transfers between devices with their start and end apart: 13, of which 6 were waited for; matrix products, arithmetic and copies ran while one was open for 30% of the time, Pallas kernels for 17%

profile of v1, /device:TPU:0, one launch (start us, length us, event | category | flops | bytes accessed | tf_op | source)
XLA Modules:
  0.0 2342.6 jit_solution(7452800095043020065)
XLA Ops:
  10.0 0.7 min.26
  11.2 1.7 fusion.9
  13.6 15.8 select_reduce_fusion.1
  29.6 5.2 fusion.8
  34.8 1.2 select_reduce_fusion.2
  36.6 15.9 select_reduce_fusion
  53.5 0.8 pad_maximum_fusion.2
  54.3 5.4 all-to-all-start
  59.7 1.5 collective-permute-start
  61.7 1.5 collective-permute-start.2
  63.2 11.7 fusion.19
  75.0 10.7 fusion.20
  85.7 19.8 multiply_convert_fusion.6
  105.5 14.6 convolution_bitcast_fusion.1
  120.2 11.0 convolution_bitcast_fusion
  131.2 9.5 fusion.21
  140.7 9.5 convert_add_fusion.refs_4_
  150.2 14.5 add_add_fusion
  164.7 10.2 fusion.22
  175.6 0.7 reshape.133.refs_0_
  177.4 65.1 %all-gather.3.cloned.1.call-done.refs_2_ = bf16[16384,1536]{1,0:T(8,128)(2,1)} async-done(((bf16[2048,1536]{1,0:T(8,128)(2,1)}), bf16[16384,1536]{1,0:T(8,128)(2,1)}) %all-gather.3.cloned.1.call-update) | async-done | bytes 50331664 | tf_op jit(solution)/shard_map/all_gather | solution.py:299
  242.5 82.0 %gather_rows.2 = (bf16[4,8,240,1536]{3,2,1,0:T(8,128)(2,1)}, bf16[4,8,240,1536]{3,2,1,0:T(8,128)(2,1)}) custom-call(s32[15360]{0:T(1024)} %reshape.133.refs_0_, s32[64]{0:T(128)} %convert_element_type.105.refs_1_, bf16[16384,1536]{1,0:T(8,128)(2,1)} %all-gather.3.cloned.1.call-done.refs_2_), custom_call_target="tpu_custom_call" | custom-call | flops 20000000000 | bytes 100000000 | tf_op jit(solution)/shard_map/gather_rows/pallas_call | solution.py:81
  324.5 22.0 fusion.23
  346.4 29.5 %multiply_convert_fusion.5 = (bf16[4,1920,512]{2,1,0:T(8,128)(2,1)}, f32[4,1920,512]{2,1,0:T(8,128)}) fusion(f32[4,1920,512]{2,1,0:T(8,128)} %fusion.23, bf16[4,1920,1536]{2,1,0:T(8,128)(2,1)} %bitcast.128, bf16[4,1536,512]{2,1,0:T(8,128)(2,1)} %param.15), kind=kOutput, calls=%fused_computation.20 | convolution fusion | flops 12103188480 | bytes 69206016 | tf_op jit(solution)/shard_map/erd,edf->erf/dot_general | solution.py:253
  376.0 19.5 convolution_convert_fusion.1
  395.5 22.1 fusion.24
  417.6 29.7 %multiply_convert_fusion.4 = (bf16[4,1920,512]{2,1,0:T(8,128)(2,1)}, f32[4,1920,512]{2,1,0:T(8,128)}) fusion(f32[4,1920,512]{2,1,0:T(8,128)} %fusion.24, bf16[4,1920,1536]{2,1,0:T(8,128)(2,1)} %bitcast.134, bf16[4,1536,512]{2,1,0:T(8,128)(2,1)} %collective-permute-done.1), kind=kOutput, calls=%fused_computation.17 | convolution fusion | flops 12103188480 | bytes 69206016 | tf_op jit(solution)/shard_map/erd,edf->erf/dot_general | solution.py:253
  447.3 20.4 collective-permute-done.2
  467.6 20.3 convolution_convert_fusion
  487.9 31.9 %copy_bitcast_fusion.1 = bf16[8,2,4,240,1536]{4,3,2,1,0:T(8,128)(2,1)} fusion(bf16[1,4,8,240,1536]{4,3,2,1,0:T(8,128)(2,1)} %bitcast.119, bf16[1,4,8,240,1536]{4,3,2,1,0:T(8,128)(2,1)} %bitcast.116), kind=kLoop, calls=%fused_computation.6 | loop fusion | flops 23592960 | bytes 94371840 | tf_op jit(solution)/shard_map/transpose | solution.py:334
  519.8 8.7 all-to-all-start.1
  528.6 0.8 reshape.137.refs_2_
  529.3 85.6 %gather_rows.3 = (bf16[4,8,240,1536]{3,2,1,0:T(8,128)(2,1)}, bf16[4,8,240,1536]{3,2,1,0:T(8,128)(2,1)}) custom-call(s32[15360]{0:T(1024)} %reshape.133.refs_0_, s32[64]{0:T(128)} %convert_element_type.105.refs_1_, f32[15360]{0:T(1024)} %reshape.137.refs_2_, bf16[16384,1536]{1,0:T(8,128)(2,1)} %all-gather.5.cloned.1.call-done.refs_3_), custom_call_target="tpu_custom_call" | custom-call | flops 20000000000 | bytes 100000000 | tf_op jit(solution)/shard_map/gather_rows/pallas_call | solution.py:81
  614.9 29.6 %multiply_convert_fusion.2 = (bf16[4,1920,512]{2,1,0:T(8,128)(2,1)}, bf16[4,1920,512]{2,1,0:T(8,128)(2,1)}) fusion(f32[4,1920,512]{2,1,0:T(8,128)} %fusion.23, f32[4,1920,512]{2,1,0:T(8,128)} %get-tuple-element.117, bf16[4,1920,1536]{2,1,0:T(8,128)(2,1)} %bitcast.131, bf16[4,512,1536]{2,1,0:T(8,128)(2,1)} %param.16), kind=kOutput, calls=%fused_computation.15 | convolution fusion | flops 12130713600 | bytes 77070336 | tf_op jit(solution)/shard_map/erd,efd->erf/dot_general | solution.py:264
  644.5 23.9 %fusion.25 = f32[4,1920,1536]{2,1,0:T(8,128)} fusion(bf16[4,1920,512]{2,1,0:T(8,128)(2,1)} %get-tuple-element.106, bf16[4,1536,512]{2,1,0:T(8,128)(2,1)} %param.14), kind=kOutput, calls=%fused_computation.88 | convolution fusion | flops 12079595520 | bytes 61341696 | tf_op jit(solution)/shard_map/erf,edf->erd/dot_general | solution.py:275
  668.4 29.8 %multiply_convert_fusion.1 = (bf16[4,1920,512]{2,1,0:T(8,128)(2,1)}, bf16[4,1920,512]{2,1,0:T(8,128)(2,1)}) fusion(f32[4,1920,512]{2,1,0:T(8,128)} %fusion.24, f32[4,1920,512]{2,1,0:T(8,128)} %get-tuple-element.115, bf16[4,1920,1536]{2,1,0:T(8,128)(2,1)} %bitcast.137, bf16[4,512,1536]{2,1,0:T(8,128)(2,1)} %collective-permute-done.2), kind=kOutput, calls=%fused_computation.14 | convolution fusion | flops 12130713600 | bytes 77070336 | tf_op jit(solution)/shard_map/erd,efd->erf/dot_general | solution.py:264
  698.2 24.1 %fusion.26 = f32[4,1920,1536]{2,1,0:T(8,128)} fusion(bf16[4,1920,512]{2,1,0:T(8,128)(2,1)} %get-tuple-element.108, bf16[4,1536,512]{2,1,0:T(8,128)(2,1)} %collective-permute-done.1), kind=kOutput, calls=%fused_computation.89 | convolution fusion | flops 12079595520 | bytes 61341696 | tf_op jit(solution)/shard_map/erf,edf->erd/dot_general | solution.py:275
  722.3 29.4 %add_convert_fusion.1 = bf16[4,1920,1536]{2,1,0:T(8,128)(2,1)} fusion(f32[4,1920,1536]{2,1,0:T(8,128)} %fusion.25, bf16[4,1920,512]{2,1,0:T(8,128)(2,1)} %get-tuple-element.105, bf16[4,1536,512]{2,1,0:T(8,128)(2,1)} %param.15), kind=kOutput, calls=%fused_computation.8 | convolution fusion | flops 12103188480 | bytes 84934656 | tf_op jit(solution)/shard_map/erf,edf->erd/dot_general | solution.py:275
  751.6 29.4 %add_convert_fusion = bf16[4,1920,1536]{2,1,0:T(8,128)(2,1)} fusion(f32[4,1920,1536]{2,1,0:T(8,128)} %fusion.26, bf16[4,1920,512]{2,1,0:T(8,128)(2,1)} %get-tuple-element.107, bf16[4,1536,512]{2,1,0:T(8,128)(2,1)} %collective-permute-done), kind=kOutput, calls=%fused_computation.7 | convolution fusion | flops 12103188480 | bytes 84934656 | tf_op jit(solution)/shard_map/erf,edf->erd/dot_general | solution.py:275
  781.0 31.8 %copy_bitcast_fusion = bf16[8,2,4,240,1536]{4,3,2,1,0:T(8,128)(2,1)} fusion(bf16[1,4,8,240,1536]{4,3,2,1,0:T(8,128)(2,1)} %bitcast.118, bf16[1,4,8,240,1536]{4,3,2,1,0:T(8,128)(2,1)} %bitcast.117), kind=kLoop, calls=%fused_computation.5 | loop fusion | flops 23592960 | bytes 94371840 | tf_op jit(solution)/shard_map/transpose | solution.py:334
  812.8 225.5 %all-to-all-done.1 = bf16[8,2,4,240,1536]{4,3,2,1,0:T(8,128)(2,1)} async-done(((bf16[8,2,4,240,1536]{4,3,2,1,0:T(8,128)(2,1)}), bf16[8,2,4,240,1536]{4,3,2,1,0:T(8,128)(2,1)}, u32[]{:S(2)}, u32[]{:S(2)}) %all-to-all-start.1) | async-done | bytes 47185952 | tf_op jit(solution)/shard_map/all_to_all | solution.py:302
  1038.3 8.2 all-to-all-start.2
  1046.6 21.5 fusion.27
  1068.1 1.5 collective-permute-start.3
  1069.6 21.4 fusion.28
  1091.6 21.9 fusion.29
  1113.4 1.5 collective-permute-start.5
  1114.9 0.7 reshape_reshape.9.refs_0_
  1115.7 0.8 reshape_reshape.11.refs_2_
  1117.1 275.1 %collective-permute-done.3 = f32[4,1536,512]{2,1,0:T(8,128)} collective-permute-done((f32[4,1536,512]{2,1,0:T(8,128)}, f32[4,1536,512]{2,1,0:T(8,128)}, u32[]{:S(2)}, u32[]{:S(2)}) %collective-permute-start.3) | collective-permute-done | bytes 12582944 | tf_op jit(solution)/shard_map/ppermute | solution.py:296
  1392.2 22.3 add_convert_fusion.4
  1414.5 348.5 %collective-permute-done.4 = f32[4,1536,512]{2,1,0:T(8,128)} collective-permute-done((f32[4,1536,512]{2,1,0:T(8,128)}, f32[4,1536,512]{2,1,0:T(8,128)}, u32[]{:S(2)}, u32[]{:S(2)}) %collective-permute-start.4) | collective-permute-done | bytes 12582944 | tf_op jit(solution)/shard_map/ppermute | solution.py:296
  1763.0 22.3 add_convert_fusion.3
  1785.3 246.7 %collective-permute-done.5 = f32[4,512,1536]{2,1,0:T(8,128)} collective-permute-done((f32[4,512,1536]{2,1,0:T(8,128)}, f32[4,512,1536]{2,1,0:T(8,128)}, u32[]{:S(2)}, u32[]{:S(2)}) %collective-permute-start.5) | collective-permute-done | bytes 12582944 | tf_op jit(solution)/shard_map/ppermute | solution.py:296
  2032.0 24.9 %add_convert_fusion.2 = bf16[4,512,1536]{2,1,0:T(8,128)(2,1)} fusion(f32[4,512,1536]{2,1,0:T(8,128)} %collective-permute-done.5, bf16[4,1920,512]{2,1,0:T(8,128)(2,1)} %get-tuple-element.116, bf16[4,1920,1536]{2,1,0:T(8,128)(2,1)} %bitcast.132), kind=kOutput, calls=%fused_computation.23 | convolution fusion | flops 12085886976 | bytes 50331648 | tf_op jit(solution)/shard_map/erf,erd->efd/dot_general | solution.py:262
  2056.9 131.9 %combine_dots.1 = (bf16[2048,1536]{1,0:T(8,128)(2,1)}, f32[16384,128]{1,0:T(8,128)}) custom-call(s32[15360]{0:T(1024)} %reshape_reshape.9.refs_0_, s32[64]{0:T(128)} %reshape_reshape.10.refs_1_, f32[15360]{0:T(1024)} %reshape_reshape.11.refs_2_, bf16[64,240,1536]{2,1,0:T(8,128)(2,1)} %bitcast.16.refs_3_, f32[2048,1536]{1,0:T(8,128)} %convert_add_fusion.refs_4_, ...), custom_call_target="tpu_custom_call" | custom-call | flops 20000000000 | bytes 100000000 | tf_op jit(solution)/shard_map/combine_dots/pallas_call | solution.py:178
  2188.9 4.7 reduce_sum.89
  2195.0 4.7 convolution_bitcast_fusion.2
  2199.7 11.0 convolution_add_fusion.refs_3_
  2210.7 104.1 %combine_rows.1 = bf16[2048,1536]{1,0:T(8,128)(2,1)} custom-call(s32[15360]{0:T(1024)} %reshape_reshape.9.refs_0_, s32[64]{0:T(128)} %reshape_reshape.10.refs_1_, bf16[64,240,1536]{2,1,0:T(8,128)(2,1)} %bitcast.22.refs_2_, f32[2048,1536]{1,0:T(8,128)} %convolution_add_fusion.refs_3_), custom_call_target="tpu_custom_call" | custom-call | flops 20000000000 | bytes 100000000 | tf_op jit(solution)/shard_map/combine_rows/pallas_call | solution.py:178
  2314.9 6.6 copy.116
  2321.4 6.7 copy.117
  2328.1 1.8 copy.135
  2329.9 5.9 copy.136
  (104 shorter events, 10.7 us)
Async XLA Ops:
  7.2 78.5 %copy-start = (bf16[1024,1536]{1,0:T(8,128)(2,1)S(1)}, bf16[1024,1536]{1,0:T(8,128)(2,1)}, u32[]{:S(2)}) copy-start(bf16[1024,1536]{1,0:T(8,128)(2,1)} %param.19) | copy-start | bytes 9437188
  7.2 1.5 copy-start.4
  7.2 235.3 %all-gather.3.cloned.1.call-start = ((), (), s32[]{:S(2)}) async-start(), calls=%async_computation.3 | async-start | bytes 56623104 | tf_op jit(solution)/shard_map/all_gather | solution.py:299
  7.9 21.7 copy-start.12
  8.0 521.4 %all-gather.5.cloned.1.call-start = ((), (), s32[]{:S(2)}) async-start(), calls=%async_computation.4 | async-start | bytes 56623104 | tf_op jit(solution)/shard_map/all_gather | solution.py:299
  9.4 0.5 copy-start.17
  12.8 0.8 copy-start.2
  29.4 7.2 copy-start.3
  29.6 24.7 %copy-start.6 = (s32[4,2,2,4,240]{4,3,2,1,0:T(4,128)}, s32[4,2,2,4,240]{4,3,2,1,0:T(4,128)S(1)}, u32[]{:S(2)}) copy-start(s32[4,2,2,4,240]{4,3,2,1,0:T(4,128)S(1)} %copy.97) | copy-start | bytes 184324
  36.0 0.6 copy-start.14
  52.6 1.7 copy-start.8
  54.3 120.6 %all-to-all-start = ((f32[8,2,4,481]{3,2,1,0:T(4,128)}), f32[8,2,4,481]{3,2,1,0:T(4,128)S(1)}, u32[]{:S(2)}, u32[]{:S(2)}) async-start(f32[8,2,4,481]{3,2,1,0:T(4,128)} %pad_maximum_fusion.2), calls=%async_computation | async-start | bytes 262144 | tf_op jit(solution)/shard_map/all_to_all | solution.py:302
  59.7 15.3 copy-start.19
  59.7 335.8 %collective-permute-start = (bf16[4,1536,512]{2,1,0:T(8,128)(2,1)}, bf16[4,1536,512]{2,1,0:T(8,128)(2,1)}, u32[]{:S(2)}, u32[]{:S(2)}) collective-permute-start(bf16[4,1536,512]{2,1,0:T(8,128)(2,1)} %param.14), channel_id=1, source_target_pairs={{0,2},{1,3},{2,0},{3,1},{4,6},{5,7},{6,4},{7,5},{8,10},{9,11},{10,... | collective-permute-start | bytes 18874376 | tf_op jit(solution)/shard_map/ppermute | solution.py:296
  61.2 356.3 %collective-permute-start.1 = (bf16[4,1536,512]{2,1,0:T(8,128)(2,1)}, bf16[4,1536,512]{2,1,0:T(8,128)(2,1)}, u32[]{:S(2)}, u32[]{:S(2)}) collective-permute-start(bf16[4,1536,512]{2,1,0:T(8,128)(2,1)} %param.15), channel_id=1, source_target_pairs={{0,2},{1,3},{2,0},{3,1},{4,6},{5,7},{6,4},{7,5},{8,10},{9,11},{10,... | collective-permute-start | bytes 18874376 | tf_op jit(solution)/shard_map/ppermute | solution.py:296
  61.7 405.9 %collective-permute-start.2 = (bf16[4,512,1536]{2,1,0:T(8,128)(2,1)}, bf16[4,512,1536]{2,1,0:T(8,128)(2,1)}, u32[]{:S(2)}, u32[]{:S(2)}) collective-permute-start(bf16[4,512,1536]{2,1,0:T(8,128)(2,1)} %param.16), channel_id=1, source_target_pairs={{0,2},{1,3},{2,0},{3,1},{4,6},{5,7},{6,4},{7,5},{8,10},{9,11},{10,... | collective-permute-start | bytes 18874376 | tf_op jit(solution)/shard_map/ppermute | solution.py:296
  105.5 14.6 copy-start.21
  120.1 11.0 copy-start.18
  120.2 11.0 copy-start.22
  120.2 20.6 slice-start
  131.2 9.5 slice-start.1
  131.2 9.5 copy-start.20
  131.2 19.0 slice-start.2
  140.7 9.5 slice-start.3
  519.8 8.8 copy-start.11
  519.8 518.5 %all-to-all-start.1 = ((bf16[8,2,4,240,1536]{4,3,2,1,0:T(8,128)(2,1)}), bf16[8,2,4,240,1536]{4,3,2,1,0:T(8,128)(2,1)}, u32[]{:S(2)}, u32[]{:S(2)}) async-start(bf16[8,2,4,240,1536]{4,3,2,1,0:T(8,128)(2,1)} %copy_bitcast_fusion.1), calls=%async_computation.1 | async-start | bytes 94371840 | tf_op jit(solution)/shard_map/all_to_all | solution.py:302
  1038.3 1172.4 %all-to-all-start.2 = ((bf16[8,2,4,240,1536]{4,3,2,1,0:T(8,128)(2,1)}), bf16[8,2,4,240,1536]{4,3,2,1,0:T(8,128)(2,1)}, u32[]{:S(2)}, u32[]{:S(2)}) async-start(bf16[8,2,4,240,1536]{4,3,2,1,0:T(8,128)(2,1)} %copy_bitcast_fusion), calls=%async_computation.2 | async-start | bytes 94371840 | tf_op jit(solution)/shard_map/all_to_all | solution.py:302
  1046.5 1153.2 %all-reduce.6.cloned.1.call-start = ((), (), s32[]{:S(2)}) async-start(), calls=%async_computation.6 | async-start | bytes 37748736 | tf_op jit(solution)/shard_map/psum | solution.py:344
  1068.1 324.1 %collective-permute-start.3 = (f32[4,1536,512]{2,1,0:T(8,128)}, f32[4,1536,512]{2,1,0:T(8,128)}, u32[]{:S(2)}, u32[]{:S(2)}) collective-permute-start(f32[4,1536,512]{2,1,0:T(8,128)} %fusion.27), channel_id=1, source_target_pairs={{0,2},{1,3},{2,0},{3,1},{4,6},{5,7},{6,4},{7,5},{8,10},{9,11},{10,... | collective-permute-start | bytes 37748744 | tf_op jit(solution)/shard_map/ppermute | solution.py:296
  1091.0 23.9 %copy-start.7 = (s32[4,2,2,4,240]{4,3,2,1,0:T(4,128)S(1)}, s32[4,2,2,4,240]{4,3,2,1,0:T(4,128)}, u32[]{:S(2)}) copy-start(s32[4,2,2,4,240]{4,3,2,1,0:T(4,128)} %copy-done.6) | copy-start | bytes 184324
  1091.0 24.7 %copy-start.9 = (f32[4,2,2,4,240]{4,3,2,1,0:T(4,128)S(1)}, f32[4,2,2,4,240]{4,3,2,1,0:T(4,128)}, u32[]{:S(2)}) copy-start(f32[4,2,2,4,240]{4,3,2,1,0:T(4,128)} %copy-done.8) | copy-start | bytes 184324
  1091.0 25.4 %copy-start.16 = (s32[4,2,2,4,1]{3,0,4,2,1:T(4,128)S(1)}, s32[4,2,2,4,1]{3,0,4,2,1:T(4,128)}, u32[]{:S(2)}) copy-start(s32[4,2,2,4,1]{3,0,4,2,1:T(4,128)} %get-tuple-element.104) | copy-start | bytes 772
  1091.0 672.0 %collective-permute-start.4 = (f32[4,1536,512]{2,1,0:T(8,128)}, f32[4,1536,512]{2,1,0:T(8,128)}, u32[]{:S(2)}, u32[]{:S(2)}) collective-permute-start(f32[4,1536,512]{2,1,0:T(8,128)} %fusion.28), channel_id=1, source_target_pairs={{0,2},{1,3},{2,0},{3,1},{4,6},{5,7},{6,4},{7,5},{8,10},{9,11},{10,... | collective-permute-start | bytes 37748744 | tf_op jit(solution)/shard_map/ppermute | solution.py:296
  1113.4 918.6 %collective-permute-start.5 = (f32[4,512,1536]{2,1,0:T(8,128)}, f32[4,512,1536]{2,1,0:T(8,128)}, u32[]{:S(2)}, u32[]{:S(2)}) collective-permute-start(f32[4,512,1536]{2,1,0:T(8,128)} %fusion.29), channel_id=1, source_target_pairs={{0,2},{1,3},{2,0},{3,1},{4,6},{5,7},{6,4},{7,5},{8,10},{9,11},{10,... | collective-permute-start | bytes 37748744 | tf_op jit(solution)/shard_map/ppermute | solution.py:296
  1117.1 1211.1 %all-reduce.4.cloned.1.call-start = ((), (), s32[]{:S(2)}) async-start(), calls=%async_computation.5 | async-start | bytes 786432 | tf_op jit(solution)/shard_map/psum | solution.py:363
  2188.9 5.6 copy-start.10
  2188.9 5.6 copy-start.15
  2188.9 5.7 copy-start.5
  2188.9 10.9 copy-start.13
  2321.4 14.4 copy-start.1
Sparse Core Ops, SparseCore 0:
  9.9 232.5 all-gather.2
  244.4 228.3 all-gather.4
  1117.2 607.7 all-reduce.5
  2199.9 65.9 all-reduce.3
